TPU v7x, 32 devices: a whole 2x2x4 slice. The times are simulated.
32 devices in a mesh: tp: 8 (over z, core), fs: 4 (over y, x).
Axes of the slice: x: 2, y: 2, z: 4, core: 2. Of those that a mesh axis runs over, the one named last changes fastest.
Arguments:
- tokens: bfloat16 [128, 8192], P(('tp', 'fs')), may hold values from -6 to 6
- gate_weight: bfloat16 [8192, 29568], P('fs', 'tp'), may hold values from -0.0625 to 0.0625
- up_weight: bfloat16 [8192, 29568], P('fs', 'tp'), may hold values from -0.0625 to 0.0625
- down_weight: bfloat16 [29568, 8192], P('tp', 'fs'), may hold values from -0.046875 to 0.046875
Outputs:
- mixed: bfloat16 [128, 8192], P(None, ('fs', 'tp'))
All inputs are finite; a program needn't handle non-finite values.
Results may differ from a plain program's by a relative error of at most 0.0049.
Values may be sent and summed in bfloat16 or wider, within the bound.
A program may use at most 128 MiB of HBM per device.

v0:
```python
import jax
import jax.numpy as jnp
from jax import lax
from jax.sharding import PartitionSpec as P


def body(tokens, gate_weight, up_weight, down_weight):
    by_feature = lax.all_to_all(tokens, "fs", split_axis=1, concat_axis=0, tiled=True)
    feature_rows = lax.all_gather(by_feature, "tp", axis=0, tiled=True)
    gate_part = jnp.dot(feature_rows, gate_weight, preferred_element_type=jnp.float32)
    up_part = jnp.dot(feature_rows, up_weight, preferred_element_type=jnp.float32)
    gate, up = (
        lax.psum_scatter(gate_part, "fs", scatter_dimension=1, tiled=True),
        lax.psum_scatter(up_part, "fs", scatter_dimension=1, tiled=True),
    )
    hidden = (jax.nn.silu(gate) * up).astype(jnp.bfloat16)
    hidden_all = lax.all_gather(hidden, "fs", axis=1, tiled=True)
    partial_out = jnp.dot(hidden_all, down_weight, preferred_element_type=jnp.float32)
    summed = lax.psum_scatter(partial_out, "tp", scatter_dimension=1, tiled=True)
    return summed.astype(jnp.bfloat16)


def solution(mesh):
    return jax.shard_map(
        body,
        mesh=mesh,
        in_specs=(P(("tp", "fs"), None), P("fs", "tp"), P("fs", "tp"), P("tp", "fs")),
        out_specs=P(None, ("fs", "tp")),
        check_vma=False,
    )
```

profile of v0, /device:TPU:0, one launch (start us, length us, event | category | flops | bytes accessed | tf_op | source)
XLA Modules:
  0.0 184.2 jit_solution(5929641926974322343)
XLA Ops:
  6.5 0.0 reduce-scatter.6.cloned.1.call-start
  6.5 10.0 %all_to_all.19 = bf16[4,4,2048]{2,0,1:T(4,128)(2,1)S(1)} all-to-all(bf16[4,4,2048]{2,0,1:T(4,128)(2,1)} %bitcast.19), channel_id=1, replica_groups=mesh['tp'=8,'fs'=4] {'fs'}, dimensions={1} | all-to-all | bytes 131072 | tf_op jit(solution)/shard_map/all_to_all | solution.py:8
  16.6 0.0 copy-start
  16.6 15.1 %all_gather.6 = bf16[128,2048]{1,0:T(8,128)(2,1)S(1)} all-gather(bf16[16,2048]{1,0:T(8,128)(2,1)S(1)} %all_to_all.17), channel_id=1, replica_groups=mesh['tp'=8,'fs'=4] {'tp'}, dimensions={0}, use_global_device_ids=true | all-gather | bytes 589824 | tf_op jit(solution)/shard_map/all_gather | solution.py:9
  31.8 7.6 %fusion.5 = f32[128,3696]{0,1:T(8,128)S(1)} fusion(bf16[128,2048]{1,0:T(8,128)(2,1)S(1)} %all_gather.6, bf16[2048,3696]{0,1:T(8,128)(2,1)} %param.5), kind=kOutput, calls=%fused_computation.3 | convolution fusion | flops 1937768448 | bytes 17555456 | tf_op jit(solution)/shard_map/dot_general | solution.py:10
  39.3 0.0 copy-done
  39.3 0.0 copy-start.1
  39.4 5.6 %fusion.6 = f32[128,3696]{0,1:T(8,128)} fusion(bf16[128,2048]{1,0:T(8,128)(2,1)S(1)} %all_gather.6, bf16[2048,3696]{0,1:T(8,128)(2,1)S(1)} %copy-done), kind=kOutput, calls=%fused_computation.4 | convolution fusion | flops 1937768448 | bytes 17555456 | tf_op jit(solution)/shard_map/dot_general | solution.py:11
  44.9 67.6 %fusion.4 = (f32[128,928]{0,1:T(8,128)S(1)}, f32[128,928]{0,1:T(8,128)S(1)}) fusion(f32[128,3696]{0,1:T(8,128)} %fusion.6, f32[128,3696]{0,1:T(8,128)S(1)} %fusion.5), kind=kCustom, calls=%all-reduce-scatter.2 | all-reduce-scatter fusion | flops 950273 | bytes 4735488
  112.6 1.7 collective-permute-start
  114.3 4.3 %collective-permute-start.1 = (f32[128,12]{0,1:T(8,128)S(1)}, f32[128,12]{0,1:T(8,128)S(1)}, u32[]{:S(2)}, u32[]{:S(2)}) collective-permute-start(f32[128,12]{0,1:T(8,128)S(1)} %slice.1), channel_id=1, source_target_pairs={{0,1},{1,2},{2,3},{4,5},{5,6},{6,7},{8,9},{9,10},{10,11},{12,13},{... | collective-permute-start | bytes 18440
  118.6 0.0 copy-done.1
  118.6 0.6 dynamic-slice.6
  119.9 0.0 collective-permute-done
  119.9 1.1 concatenate
  121.0 0.0 collective-permute-done.1
  121.0 1.1 concatenate.1
  122.1 0.2 fusion.3
  122.3 12.0 %all-gather = bf16[4,924,128]{2,1,0:T(8,128)(2,1)S(1)} all-gather(bf16[1,924,128]{2,1,0:T(8,128)(2,1)S(1)} %fusion.3), channel_id=1, replica_groups=mesh['tp'=8,'fs'=4] {'fs'}, dimensions={0}, use_global_device_ids=true | all-gather | bytes 1182720 | tf_op jit(solution)/shard_map/all_gather | solution.py:17
  134.3 0.2 reshape.4
  134.5 8.5 %fusion.7 = f32[128,2048]{1,0:T(8,128)} fusion(bf16[3696,128]{1,0:T(8,128)(2,1)S(1)} %reshape.4, bf16[3696,2048]{1,0:T(8,128)(2,1)} %param.7), kind=kOutput, calls=%fused_computation.5 | convolution fusion | flops 1937768448 | bytes 17133568 | tf_op jit(solution)/shard_map/dot_general | solution.py:18
  143.0 0.0 reduce-scatter.6.cloned.1.call-update
  143.0 32.8 %reduce-scatter.6.cloned.1.call-done = f32[128,256]{1,0:T(8,128)} async-done(((f32[128,2048]{1,0:T(8,128)}), f32[128,256]{1,0:T(8,128)}) %reduce-scatter.6.cloned.1.call-update) | async-done | bytes 131088 | tf_op jit(solution)/shard_map/reduce_scatter | solution.py:19
  175.8 1.5 convert_element_type.7
  (3 shorter events, 0.0 us)
Async XLA Ops:
  6.5 169.3 %reduce-scatter.6.cloned.1.call-start = ((), (), s32[]{:S(2)}) async-start(), calls=%async_computation.2 | async-start | bytes 1179648 | tf_op jit(solution)/shard_map/reduce_scatter | solution.py:19
  16.6 22.7 %copy-start = (bf16[2048,3696]{0,1:T(8,128)(2,1)S(1)}, bf16[2048,3696]{0,1:T(8,128)(2,1)}, u32[]{:S(2)}) copy-start(bf16[2048,3696]{0,1:T(8,128)(2,1)} %param.6) | copy-start | bytes 45416452
  39.3 79.3 %copy-start.1 = (u32[32]{0:T(128)S(1)}, u32[32]{0:T(128)}, u32[]{:S(2)}) copy-start(u32[32]{0:T(128)} %constant.6) | copy-start | bytes 388
  112.6 7.3 %collective-permute-start = (f32[128,12]{0,1:T(8,128)S(1)}, f32[128,12]{0,1:T(8,128)S(1)}, u32[]{:S(2)}, u32[]{:S(2)}) collective-permute-start(f32[128,12]{0,1:T(8,128)S(1)} %slice), channel_id=1, source_target_pairs={{0,1},{1,2},{2,3},{4,5},{5,6},{6,7},{8,9},{9,10},{10,11},{12,13},{... | collective-permute-start | bytes 18440
  114.3 6.7 %collective-permute-start.1 = (f32[128,12]{0,1:T(8,128)S(1)}, f32[128,12]{0,1:T(8,128)S(1)}, u32[]{:S(2)}, u32[]{:S(2)}) collective-permute-start(f32[128,12]{0,1:T(8,128)S(1)} %slice.1), channel_id=1, source_target_pairs={{0,1},{1,2},{2,3},{4,5},{5,6},{6,7},{8,9},{9,10},{10,11},{12,13},{... | collective-permute-start | bytes 18440
Sparse Core Ops, SparseCore 0:
  143.1 32.6 reduce-scatter.5
where the time goes:
time: 185 us; the launch traced here: 184 us
  blocking collectives  105 us (57%)
  waiting for transfers between devices  32.9 us (18%)
  matrix products  21.6 us (12%)
  between operations  14.2 us (8%)
  starting transfers between devices  6.01 us (3%)
  local copies, waits for them, and re-layouts  3.02 us (2%)
    unnamed x1, blocking collectives  67.6 us
    reduce_scatter x1, waiting for transfers between devices, body(): lax.psum_scatter(partial_out, 'tp', scatter_dimension=1, tiled=True)  32.8 us
    all_gather x1, blocking collectives, body(): feature_rows = lax.all_gather(by_feature, 'tp', axis=0, tiled=True)  15.1 us
    all_gather x1, blocking collectives, body(): hidden_all = lax.all_gather(hidden, 'fs', axis=1, tiled=True)  12 us
    all_to_all x1, blocking collectives, body(): lax.all_to_all(tokens, 'fs', split_axis=1, concat_axis=0, tiled=True)  10 us
    dot_general x1, matrix products, body(): jnp.dot(hidden_all, down_weight, preferred_element_type=jnp.float32)  8.5 us
    dot_general x1, matrix products, body(): jnp.dot(feature_rows, gate_weight, preferred_element_type=jnp.float32)  7.58 us
    unnamed x2, starting transfers between devices  6.01 us
  transfers between devices with their start and end apart: 3, of which 1 were waited for; matrix products, arithmetic and copies ran while one was open for 1% of the time, Pallas kernels for 0%

commit v1 on v0

--- a/solution.py
+++ b/solution.py
@@ -14,7 +14,12 @@
         lax.psum_scatter(up_part, "fs", scatter_dimension=1, tiled=True),
     )
     hidden = (jax.nn.silu(gate) * up).astype(jnp.bfloat16)
-    hidden_all = lax.all_gather(hidden, "fs", axis=1, tiled=True)
+    ring = [hidden]
+    for hop in range(3):
+        ring.append(lax.ppermute(ring[-1], "fs", [(dev, (dev + 1) % 4) for dev in range(4)]))
+    hidden_all = jnp.roll(
+        jnp.concatenate(ring[::-1], axis=1), (lax.axis_index("fs") + 1) * ring[0].shape[1], axis=1
+    )
     partial_out = jnp.dot(hidden_all, down_weight, preferred_element_type=jnp.float32)
     summed = lax.psum_scatter(partial_out, "tp", scatter_dimension=1, tiled=True)
     return summed.astype(jnp.bfloat16)

time: 185 us -> 200 us (1.081)
  waiting for transfers between devices: 32.9 us -> 53.2 us
  blocking collectives: 105 us -> 92.8 us
  local copies, waits for them, and re-layouts: 3.02 us -> 8.72 us
    ppermute x0 -> x3, waiting for transfers between devices: none -> 20.3 us  [body(): lax.ppermute(ring[-1], 'fs', [(dev, (dev + 1) % 4) for dev in range(4)])]
    all_gather x1 -> x0, blocking collectives: 12 us -> none  [body(): hidden_all = lax.all_gather(hidden, 'fs', axis=1, tiled=True)]
    concatenate x0 -> x1, local copies, waits for them, and re-layouts: none -> 4 us  [body(): jnp.roll(jnp.concatenate(ring[::-1], axis=1), (lax.axis_index('fs') + 1)...]
    unnamed x10 -> x9, local copies, waits for them, and re-layouts: 3 us -> 4.7 us
  transfers between devices with their start and end apart: 3 -> 6, of which waited for: 1 -> 4; matrix products, arithmetic and copies ran while one was open for 1% -> 1% of each run, Pallas kernels for 0% -> 0%
where the time goes in v1:
time: 200 us
  blocking collectives  92.8 us (46%)
  waiting for transfers between devices  53.2 us (27%)
  matrix products  21.8 us (11%)
  between operations  14.1 us (7%)
  local copies, waits for them, and re-layouts  8.72 us (4%)
  starting transfers between devices  7.26 us (4%)
    unnamed x1, blocking collectives  67.8 us
    reduce_scatter x1, waiting for transfers between devices, body(): lax.psum_scatter(partial_out, 'tp', scatter_dimension=1, tiled=True)  32.8 us
    ppermute x3, waiting for transfers between devices, body(): lax.ppermute(ring[-1], 'fs', [(dev, (dev + 1) % 4) for dev in range(4)])  20.3 us
    all_gather x1, blocking collectives, body(): feature_rows = lax.all_gather(by_feature, 'tp', axis=0, tiled=True)  15 us
    all_to_all x1, blocking collectives, body(): lax.all_to_all(tokens, 'fs', split_axis=1, concat_axis=0, tiled=True)  10 us
    dot_general x1, matrix products, body(): jnp.dot(hidden_all, down_weight, preferred_element_type=jnp.float32)  8.56 us
    dot_general x1, matrix products, body(): jnp.dot(feature_rows, gate_weight, preferred_element_type=jnp.float32)  7.73 us
    unnamed x2, starting transfers between devices  6.01 us
  transfers between devices with their start and end apart: 6, of which 4 were waited for; matrix products, arithmetic and copies ran while one was open for 1% of the time, Pallas kernels for 0%

profile of v1, /device:TPU:0, one launch (start us, length us, event | category | flops | bytes accessed | tf_op | source)
XLA Modules:
  0.0 199.7 jit_solution(17973246119653587589)
XLA Ops:
  6.5 0.0 reduce-scatter.6.cloned.1.call-start
  6.5 10.0 %all_to_all.19 = bf16[4,4,2048]{2,0,1:T(4,128)(2,1)S(1)} all-to-all(bf16[4,4,2048]{2,0,1:T(4,128)(2,1)} %bitcast.14), channel_id=1, replica_groups=mesh['tp'=8,'fs'=4] {'fs'}, dimensions={1} | all-to-all | bytes 131072 | tf_op jit(solution)/shard_map/all_to_all | solution.py:8
  16.6 15.0 %all_gather.3 = bf16[128,2048]{1,0:T(8,128)(2,1)S(1)} all-gather(bf16[16,2048]{1,0:T(8,128)(2,1)S(1)} %all_to_all.17), channel_id=1, replica_groups=mesh['tp'=8,'fs'=4] {'tp'}, dimensions={0}, use_global_device_ids=true | all-gather | bytes 589824 | tf_op jit(solution)/shard_map/all_gather | solution.py:9
  31.6 0.0 copy-start
  31.6 7.7 %fusion.7 = f32[128,3696]{0,1:T(8,128)S(1)} fusion(bf16[128,2048]{1,0:T(8,128)(2,1)S(1)} %all_gather.3, bf16[2048,3696]{0,1:T(8,128)(2,1)} %param.5), kind=kOutput, calls=%fused_computation.5 | convolution fusion | flops 1937768448 | bytes 17555456 | tf_op jit(solution)/shard_map/dot_general | solution.py:10
  39.3 1.9 copy-done
  41.2 5.6 %fusion.8 = f32[128,3696]{0,1:T(8,128)} fusion(bf16[128,2048]{1,0:T(8,128)(2,1)S(1)} %all_gather.3, bf16[2048,3696]{0,1:T(8,128)(2,1)S(1)} %copy-done), kind=kOutput, calls=%fused_computation.6 | convolution fusion | flops 1937768448 | bytes 17555456 | tf_op jit(solution)/shard_map/dot_general | solution.py:11
  46.8 0.0 copy-start.1
  46.8 67.8 %fusion.6 = (f32[128,928]{0,1:T(8,128)S(1)}, f32[128,928]{0,1:T(8,128)S(1)}) fusion(f32[128,3696]{0,1:T(8,128)} %fusion.8, f32[128,3696]{0,1:T(8,128)S(1)} %fusion.7), kind=kCustom, calls=%all-reduce-scatter.2 | all-reduce-scatter fusion | flops 950273 | bytes 4735488
  114.6 1.8 collective-permute-start.3
  116.3 4.3 %collective-permute-start.4 = (f32[128,12]{0,1:T(8,128)S(1)}, f32[128,12]{0,1:T(8,128)S(1)}, u32[]{:S(2)}, u32[]{:S(2)}) collective-permute-start(f32[128,12]{0,1:T(8,128)S(1)} %slice.1), channel_id=1, source_target_pairs={{0,1},{1,2},{2,3},{4,5},{5,6},{6,7},{8,9},{9,10},{10,11},{12,13},{... | collective-permute-start | bytes 18440
  120.6 0.0 copy-done.1
  120.6 0.6 dynamic-slice.6
  121.8 0.0 collective-permute-done.3
  121.9 1.1 concatenate.7
  123.0 0.0 collective-permute-done.4
  123.0 1.1 concatenate.8
  124.1 0.2 fusion.4
  124.3 1.2 collective-permute-start
  125.6 6.3 %collective-permute-done = bf16[128,924]{0,1:T(8,128)(2,1)S(1)} collective-permute-done((bf16[128,924]{0,1:T(8,128)(2,1)S(1)}, bf16[128,924]{0,1:T(8,128)(2,1)S(1)}, u32[]{:S(2)}, u32[]{:S(2)}) %collective-permute-start) | collective-permute-done | bytes 236576 | tf_op jit(solution)/shard_map/ppermute | solution.py:19
  131.9 0.0 collective-permute-start.1
  131.9 7.0 %collective-permute-done.1 = bf16[128,924]{0,1:T(8,128)(2,1)S(1)} collective-permute-done((bf16[128,924]{0,1:T(8,128)(2,1)S(1)}, bf16[128,924]{0,1:T(8,128)(2,1)S(1)}, u32[]{:S(2)}, u32[]{:S(2)}) %collective-permute-start.1) | collective-permute-done | bytes 236576 | tf_op jit(solution)/shard_map/ppermute | solution.py:19
  138.9 0.0 collective-permute-start.2
  138.9 7.0 %collective-permute-done.2 = bf16[128,924]{0,1:T(8,128)(2,1)S(1)} collective-permute-done((bf16[128,924]{0,1:T(8,128)(2,1)S(1)}, bf16[128,924]{0,1:T(8,128)(2,1)S(1)}, u32[]{:S(2)}, u32[]{:S(2)}) %collective-permute-start.2) | collective-permute-done | bytes 236576 | tf_op jit(solution)/shard_map/ppermute | solution.py:19
  145.9 4.0 %concatenate.6 = bf16[128,7392]{0,1:T(8,128)(2,1)S(1)} concatenate(bf16[128,924]{0,1:T(8,128)(2,1)S(1)} %collective-permute-done.2, bf16[128,924]{0,1:T(8,128)(2,1)S(1)} %collective-permute-done.1, bf16[128,924]{0,1:T(8,128)(2,1)S(1)} %collective-permute-done, bf16[128,924]{0,1:T(8,128)(2,1)S(1)} %fusion.4, bf16[128,924]{0,1:T(8,128)(2,1)S(1)} %collective-permute-done.2, ...), dimensions={1} | concatenate | bytes 3784704 | tf_op jit(solution)/shard_map/jit(_roll_dynamic)/concatenate | solution.py:20
  149.9 8.6 %fusion.2 = f32[128,2048]{1,0:T(8,128)} fusion(bf16[3696,2048]{1,0:T(8,128)(2,1)} %param.7, bf16[128,7392]{0,1:T(8,128)(2,1)S(1)} %concatenate.6, s32[]{:T(128)S(6)} %select_n.14), kind=kOutput, calls=%fused_computation | convolution fusion | flops 1937768448 | bytes 17133572 | tf_op jit(solution)/shard_map/dot_general | solution.py:23
  158.5 0.0 reduce-scatter.6.cloned.1.call-update
  158.5 32.8 %reduce-scatter.6.cloned.1.call-done = f32[128,256]{1,0:T(8,128)} async-done(((f32[128,2048]{1,0:T(8,128)}), f32[128,256]{1,0:T(8,128)}) %reduce-scatter.6.cloned.1.call-update) | async-done | bytes 131088 | tf_op jit(solution)/shard_map/reduce_scatter | solution.py:24
  191.3 1.5 convert_element_type.7
  (3 shorter events, 0.0 us)
Async XLA Ops:
  6.5 184.7 %reduce-scatter.6.cloned.1.call-start = ((), (), s32[]{:S(2)}) async-start(), calls=%async_computation.2 | async-start | bytes 1179648 | tf_op jit(solution)/shard_map/reduce_scatter | solution.py:24
  31.6 9.6 %copy-start = (bf16[2048,3696]{0,1:T(8,128)(2,1)S(1)}, bf16[2048,3696]{0,1:T(8,128)(2,1)}, u32[]{:S(2)}) copy-start(bf16[2048,3696]{0,1:T(8,128)(2,1)} %param.6) | copy-start | bytes 45416452
  46.8 73.8 %copy-start.1 = (u32[32]{0:T(128)S(1)}, u32[32]{0:T(128)}, u32[]{:S(2)}) copy-start(u32[32]{0:T(128)} %constant.33) | copy-start | bytes 388
  114.6 7.3 %collective-permute-start.3 = (f32[128,12]{0,1:T(8,128)S(1)}, f32[128,12]{0,1:T(8,128)S(1)}, u32[]{:S(2)}, u32[]{:S(2)}) collective-permute-start(f32[128,12]{0,1:T(8,128)S(1)} %slice), channel_id=1, source_target_pairs={{0,1},{1,2},{2,3},{4,5},{5,6},{6,7},{8,9},{9,10},{10,11},{12,13},{... | collective-permute-start | bytes 18440
  116.3 6.6 %collective-permute-start.4 = (f32[128,12]{0,1:T(8,128)S(1)}, f32[128,12]{0,1:T(8,128)S(1)}, u32[]{:S(2)}, u32[]{:S(2)}) collective-permute-start(f32[128,12]{0,1:T(8,128)S(1)} %slice.1), channel_id=1, source_target_pairs={{0,1},{1,2},{2,3},{4,5},{5,6},{6,7},{8,9},{9,10},{10,11},{12,13},{... | collective-permute-start | bytes 18440
  124.3 7.6 %collective-permute-start = (bf16[128,924]{0,1:T(8,128)(2,1)S(1)}, bf16[128,924]{0,1:T(8,128)(2,1)S(1)}, u32[]{:S(2)}, u32[]{:S(2)}) collective-permute-start(bf16[128,924]{0,1:T(8,128)(2,1)S(1)} %fusion.4), channel_id=1, source_target_pairs={{0,1},{1,2},{2,3},{3,0},{4,5},{5,6},{6,7},{7,4},{8,9},{9,10},{10,1... | collective-permute-start | bytes 709640 | tf_op jit(solution)/shard_map/ppermute | solution.py:19
  131.9 7.0 %collective-permute-start.1 = (bf16[128,924]{0,1:T(8,128)(2,1)S(1)}, bf16[128,924]{0,1:T(8,128)(2,1)S(1)}, u32[]{:S(2)}, u32[]{:S(2)}) collective-permute-start(bf16[128,924]{0,1:T(8,128)(2,1)S(1)} %collective-permute-done), channel_id=1, source_target_pairs={{0,1},{1,2},{2,3},{3,0},{4,5},{5,6},{6,7},{7,4},{8,9},{9,10},{10,1... | collective-permute-start | bytes 709640 | tf_op jit(solution)/shard_map/ppermute | solution.py:19
  138.9 7.0 %collective-permute-start.2 = (bf16[128,924]{0,1:T(8,128)(2,1)S(1)}, bf16[128,924]{0,1:T(8,128)(2,1)S(1)}, u32[]{:S(2)}, u32[]{:S(2)}) collective-permute-start(bf16[128,924]{0,1:T(8,128)(2,1)S(1)} %collective-permute-done.1), channel_id=1, source_target_pairs={{0,1},{1,2},{2,3},{3,0},{4,5},{5,6},{6,7},{7,4},{8,9},{9,10},{10,1... | collective-permute-start | bytes 709640 | tf_op jit(solution)/shard_map/ppermute | solution.py:19
Sparse Core Ops, SparseCore 0:
  158.6 32.6 reduce-scatter.5
